TPU v7x, 128 devices: a whole 4x4x4 slice. The times are simulated.
128 devices in a mesh: row: 8 (over y, core), col: 16 (over x, z).
Axes of the slice: x: 4, y: 4, z: 4, core: 2. Of those that a mesh axis runs over, the one named last changes fastest.
Arguments:
- matrix_in: float32 [4, 4096, 2, 8192], P(None, 'row', None, 'col'), as said below
- panel_start: int32 [1], replicated, may hold values from 0 to 29
Outputs:
- matrix_out: float32 [4, 4096, 2, 8192], P(None, 'row', None, 'col')
Inputs may be any that keep to these rules, and one draw needn't show every extreme that they name: matrix_in is symmetric and positive definite.
All inputs are finite; a program needn't handle non-finite values.
Results may differ from a plain program's by a relative error of at most 0.0001.
Values sent between devices are 32-bit elements.
No kernel may reach another device: no remote copies, remote signals or barrier semaphores. Data moves between devices by JAX's collectives and lax.ppermute only.
A program may use at most 128 MiB of HBM per device.

v0:
```python
import jax
import jax.numpy as jnp
from jax import lax
from jax.sharding import PartitionSpec as P


def picked(x, axis, root):
    return lax.dynamic_index_in_dim(lax.all_gather(x, axis), root, 0, keepdims=False)


def from_root(value, axis, source):
    kept = jnp.where(lax.axis_index(axis) == source, value, 0).astype(value.dtype)
    return lax.psum(kept, axis)


def padded_to(lines, length):
    spare = -lines.shape[0] % length
    if not spare:
        return lines
    return jnp.concatenate([lines, jnp.zeros((spare, *lines.shape[1:]), lines.dtype)])


def broadcast_by_parts(x, axis, root):
    lines = jnp.where(lax.axis_index(axis) == root, x, jnp.zeros_like(x)).reshape(
        -1, *x.shape[1:][-1:]
    )
    padded = padded_to(lines, lax.axis_size(axis))
    own = lax.psum_scatter(padded, axis, scatter_dimension=0, tiled=True)
    return lax.all_gather(own, axis, axis=0, tiled=True)[: len(lines)].reshape(x.shape)


def update(matrix, rows_part, cols_part):
    loc_rows, width, _unused_a = rows_part.shape
    loc_cols = cols_part.shape[0]
    left_panel = rows_part.reshape(loc_rows * width, width)
    right_panel = cols_part.reshape(loc_cols * width, width)
    product = lax.dot_general(
        left_panel,
        right_panel,
        (((1,), (1,)), ((), ())),
        precision=lax.Precision.HIGHEST,
        preferred_element_type=jnp.float32,
    )
    return matrix - product.reshape(loc_rows, width, loc_cols, width)


def factor_panel(matrix, panel):
    rows_dev = lax.axis_size("row")
    cols_dev = lax.axis_size("col")
    my_row = lax.axis_index("row")
    my_col = lax.axis_index("col")
    loc_rows, width, loc_cols, _unused_b = matrix.shape
    row_blocks = jnp.arange(loc_rows, dtype=jnp.int32) * rows_dev + my_row
    col_local = panel // cols_dev
    row_local = panel // rows_dev
    owner_row = panel % rows_dev
    owner_col = panel % cols_dev
    column_strip = lax.dynamic_index_in_dim(matrix, col_local, 2, keepdims=False)
    diag_raw = lax.dynamic_index_in_dim(column_strip, row_local, 0, keepdims=False)
    factor = picked(jnp.linalg.cholesky(diag_raw), "row", owner_row)
    flat_rows = column_strip.reshape(loc_rows * width, width)
    solved = jax.scipy.linalg.solve_triangular(factor, flat_rows.T, lower=True).T
    solved = solved.reshape(loc_rows, width, width)
    below_panel = (row_blocks > panel)[:, None, None]
    on_panel = (row_blocks == panel)[:, None, None]
    rows_local = jnp.where(below_panel, solved, jnp.float32(0.0))
    rows_part = from_root(rows_local, "col", owner_col)
    new_strip = jnp.where(below_panel, solved, column_strip)
    new_strip = jnp.where(on_panel, factor[None, :, :], new_strip)
    written = jnp.where(my_col == owner_col, new_strip, column_strip)
    matrix = lax.dynamic_update_index_in_dim(matrix, written, col_local, 2)
    stride_ratio = cols_dev // rows_dev
    source_row = my_col % rows_dev
    offset_pick = my_col // rows_dev
    received = broadcast_by_parts(rows_part, "row", source_row)
    grouped = received.reshape(loc_cols, stride_ratio, width, width)
    cols_part = lax.dynamic_index_in_dim(grouped, offset_pick, 1, keepdims=False)
    return (rows_part, cols_part, matrix)


def per_device(matrix_in, panel_start):
    first_panel = panel_start[0]
    matrix = matrix_in
    cols_dev = lax.axis_size("col")
    loc_rows, width, loc_cols, _unused_c = matrix.shape
    rows_first, cols_first, matrix = factor_panel(matrix, first_panel)
    next_panel = first_panel + 1
    col_next = next_panel // cols_dev
    next_strip = lax.dynamic_index_in_dim(matrix, col_next, 2, keepdims=False)
    next_piece = lax.dynamic_index_in_dim(cols_first, col_next, 0, keepdims=False)
    left_panel = rows_first.reshape(loc_rows * width, width)
    strip_product = lax.dot_general(
        left_panel,
        next_piece,
        (((1,), (1,)), ((), ())),
        precision=lax.Precision.HIGHEST,
        preferred_element_type=jnp.float32,
    )
    next_strip = next_strip - strip_product.reshape(loc_rows, width, width)
    matrix = lax.dynamic_update_index_in_dim(matrix, next_strip, col_next, 2)
    rows_second, cols_second, matrix = factor_panel(matrix, next_panel)
    skipped = (jnp.arange(loc_cols, dtype=jnp.int32) == col_next)[:, None, None]
    cols_rest = jnp.where(skipped, jnp.float32(0.0), cols_first)
    matrix = update(matrix, rows_first, cols_rest)
    matrix = update(matrix, rows_second, cols_second)
    return matrix


def solution(mesh):
    return jax.shard_map(
        per_device,
        mesh=mesh,
        in_specs=(P(None, "row", None, "col"), P()),
        out_specs=P(None, "row", None, "col"),
        check_vma=False,
    )
```

profile of v0, /device:TPU:1, one launch (start us, length us, event | category | flops | bytes accessed | tf_op | source)
XLA Modules:
  0.0 873.0 jit_solution(14277893120988400959)
XLA Ops:
  11.3 11.7 %cholesky.286 = f32[128,128]{1,0:T(8,128)S(1)} custom-call(f32[128,128]{1,0:T(8,128)S(1)} %cholesky.426), custom_call_target="Cholesky" | custom-call | tf_op jit(solution)/shard_map/jit(cholesky)/cholesky | solution.py:60
  33.7 11.7 %cholesky.305 = f32[128,128]{1,0:T(8,128)S(1)} custom-call(f32[128,128]{1,0:T(8,128)S(1)} %cholesky.430), custom_call_target="Cholesky" | custom-call | tf_op jit(solution)/shard_map/jit(cholesky)/cholesky | solution.py:60
  45.4 10.0 %custom-call.28 = f32[1,128,128]{1,2,0:T(8,128)S(1)} custom-call(f32[1,128,128]{2,1,0:T(8,128)S(1)} %get-tuple-element.63), custom_call_target="InvertDiagBlocksLowerTriangular" | custom-call | tf_op jit(solution)/shard_map/jit(cholesky)/cholesky | solution.py:60
  56.1 11.7 %cholesky.326 = f32[128,128]{1,0:T(8,128)S(1)} custom-call(f32[128,128]{1,0:T(8,128)S(1)} %cholesky.435), custom_call_target="Cholesky" | custom-call | tf_op jit(solution)/shard_map/jit(cholesky)/cholesky | solution.py:60
  78.9 11.7 %cholesky.343 = f32[128,128]{1,0:T(8,128)S(1)} custom-call(f32[128,128]{1,0:T(8,128)S(1)} %convolution_subtract_fusion.9), custom_call_target="Cholesky" | custom-call | tf_op jit(solution)/shard_map/jit(cholesky)/cholesky | solution.py:60
  109.0 40.4 %all-gather.11.cloned.1.call-done = f32[4096,512]{1,0:T(8,128)} async-done(((f32[512,512]{1,0:T(8,128)}), f32[4096,512]{1,0:T(8,128)}) %all-gather.11.cloned.1.call-update) | async-done | bytes 8388624 | tf_op jit(solution)/shard_map/all_gather | solution.py:8
  159.2 39.7 %custom-call.30 = f32[4,128,128]{1,2,0:T(8,128)S(1)} custom-call(f32[4,128,128]{2,1,0:T(8,128)S(1)} %get-tuple-element.21), custom_call_target="InvertDiagBlocksLowerTriangular" | custom-call | tf_op jit(solution)/shard_map/jit(_solve_triangular)/triangular_solve | solution.py:62
  229.5 103.3 %all-reduce.4.cloned.1.call-done = f32[4,512,512]{2,1,0:T(8,128)} async-done(((f32[4,512,512]{2,1,0:T(8,128)}), f32[4,512,512]{2,1,0:T(8,128)}) %all-reduce.4.cloned.1.call-update) | async-done | bytes 4194320 | tf_op jit(solution)/shard_map/psum | solution.py:13
  335.3 36.9 %reduce-scatter.3.cloned.1.call-done = f32[256,512]{1,0:T(8,128)} async-done(((f32[2048,512]{1,0:T(8,128)}), f32[256,512]{1,0:T(8,128)}) %reduce-scatter.3.cloned.1.call-update) | async-done | bytes 524304 | tf_op jit(solution)/shard_map/reduce_scatter | solution.py:28
  383.7 24.3 %all-gather.7.cloned.1.call-done = f32[2048,512]{1,0:T(8,128)} async-done(((f32[256,512]{1,0:T(8,128)}), f32[2048,512]{1,0:T(8,128)}) %all-gather.7.cloned.1.call-update) | async-done | bytes 4194320 | tf_op jit(solution)/shard_map/all_gather | solution.py:29
  408.0 11.0 %bitcast_dynamic-update-slice_fusion.2 = f32[4,512,2,512]{3,1,2,0:T(8,128)} fusion(f32[4,512,2,512]{3,1,2,0:T(8,128)} %select_dynamic-update-slice_fusion.1, s32[]{:T(128)S(6)} %select_n.178, f32[4,512,1,512]{3,1,2,0:T(8,128)} %constant_dynamic-slice_fusion.4, f32[4,512,512]{2,1,0:T(8,128)} %all-reduce.4.cloned.1.call-done, ...), kind=kOutput, calls=%fused_computation.11 | convolution fusion | flops 6443499520 | bytes 13631500 | tf_op jit(solution)/shard_map/dot_general | solution.py:92
  422.1 11.7 %cholesky.358 = f32[128,128]{1,0:T(8,128)S(1)} custom-call(f32[128,128]{1,0:T(8,128)S(1)} %cholesky.439), custom_call_target="Cholesky" | custom-call | tf_op jit(solution)/shard_map/jit(cholesky)/cholesky | solution.py:60
  445.1 11.7 %cholesky.377 = f32[128,128]{1,0:T(8,128)S(1)} custom-call(f32[128,128]{1,0:T(8,128)S(1)} %cholesky.443), custom_call_target="Cholesky" | custom-call | tf_op jit(solution)/shard_map/jit(cholesky)/cholesky | solution.py:60
  457.6 10.2 %custom-call.32 = f32[1,128,128]{1,2,0:T(8,128)S(1)} custom-call(f32[1,128,128]{2,1,0:T(8,128)S(1)} %get-tuple-element.53), custom_call_target="InvertDiagBlocksLowerTriangular" | custom-call | tf_op jit(solution)/shard_map/jit(cholesky)/cholesky | solution.py:60
  468.5 11.7 %cholesky.398 = f32[128,128]{1,0:T(8,128)S(1)} custom-call(f32[128,128]{1,0:T(8,128)S(1)} %cholesky.448), custom_call_target="Cholesky" | custom-call | tf_op jit(solution)/shard_map/jit(cholesky)/cholesky | solution.py:60
  491.3 11.7 %cholesky.415 = f32[128,128]{1,0:T(8,128)S(1)} custom-call(f32[128,128]{1,0:T(8,128)S(1)} %convolution_subtract_fusion.8), custom_call_target="Cholesky" | custom-call | tf_op jit(solution)/shard_map/jit(cholesky)/cholesky | solution.py:60
  512.2 45.1 %all-gather.13.cloned.1.call-done = f32[4096,512]{1,0:T(8,128)} async-done(((f32[512,512]{1,0:T(8,128)}), f32[4096,512]{1,0:T(8,128)}) %all-gather.13.cloned.1.call-update) | async-done | bytes 8388624 | tf_op jit(solution)/shard_map/all_gather | solution.py:8
  566.7 39.3 %custom-call.34 = f32[4,128,128]{1,2,0:T(8,128)S(1)} custom-call(f32[4,128,128]{2,1,0:T(8,128)S(1)} %get-tuple-element.22), custom_call_target="InvertDiagBlocksLowerTriangular" | custom-call | tf_op jit(solution)/shard_map/jit(_solve_triangular)/triangular_solve | solution.py:62
  636.8 103.3 %all-reduce.6.cloned.1.call-done = f32[4,512,512]{2,1,0:T(8,128)} async-done(((f32[4,512,512]{2,1,0:T(8,128)}), f32[4,512,512]{2,1,0:T(8,128)}) %all-reduce.6.cloned.1.call-update) | async-done | bytes 4194320 | tf_op jit(solution)/shard_map/psum | solution.py:13
  742.6 36.9 %reduce-scatter.5.cloned.1.call-done = f32[256,512]{1,0:T(8,128)} async-done(((f32[2048,512]{1,0:T(8,128)}), f32[256,512]{1,0:T(8,128)}) %reduce-scatter.5.cloned.1.call-update) | async-done | bytes 524304 | tf_op jit(solution)/shard_map/reduce_scatter | solution.py:28
  786.3 29.1 %all-gather.9.cloned.1.call-done = f32[2048,512]{1,0:T(8,128)} async-done(((f32[256,512]{1,0:T(8,128)}), f32[2048,512]{1,0:T(8,128)}) %all-gather.9.cloned.1.call-update) | async-done | bytes 4194320 | tf_op jit(solution)/shard_map/all_gather | solution.py:29
  815.5 17.0 %fusion = f32[4,512,2,512]{3,1,2,0:T(8,128)S(1)} fusion(f32[4,512,512]{2,1,0:T(8,128)} %all-reduce.6.cloned.1.call-done, f32[2,2,512,512]{3,2,1,0:T(8,128)} %bitcast.194, s32[]{:T(128)S(6)} %select_n.187), kind=kOutput, calls=%fused_computation.7 | convolution fusion | flops 12884901888 | bytes 14680068 | tf_op jit(solution)/shard_map/dot_general | solution.py:37
  832.5 18.1 %subtract_subtract_fusion = f32[4,512,2,512]{3,1,2,0:T(8,128)} fusion(f32[4,512,2,512]{3,1,2,0:T(8,128)S(1)} %fusion, f32[4,512,2,512]{3,1,2,0:T(8,128)S(1)} %copy-done, f32[4,512,512]{2,1,0:T(8,128)S(1)} %copy-done.1, f32[2,2,512,512]{3,2,1,0:T(8,128)} %bitcast.193, s32[]{:T(128)S(6)} %select_n.187, pred[2]{0:T(512)(128)(4,1)S(1)} %iota_compare_fusion.3), kind=kOutput, calls=%fused_computation.4 | convolution fusion | flops 12889620480 | bytes 31457286 | tf_op jit(solution)/shard_map/dot_general | solution.py:37
  850.6 15.4 %copy.15 = f32[4,512,2,512]{3,2,1,0:T(2,128)} copy(f32[4,512,2,512]{3,1,2,0:T(8,128)} %subtract_subtract_fusion) | data formatting | bytes 16777216 | tf_op jit(solution)/shard_map/sub | solution.py:44
  (135 shorter events, 195.1 us)
Async XLA Ops:
  6.5 142.9 %all-gather.11.cloned.1.call-start = ((), (), s32[]{:S(2)}) async-start(), calls=%async_computation.8 | async-start | bytes 9437184 | tf_op jit(solution)/shard_map/all_gather | solution.py:8
  96.0 236.8 %all-reduce.4.cloned.1.call-start = ((), (), s32[]{:S(2)}) async-start(), calls=%async_computation.2 | async-start | bytes 8388608 | tf_op jit(solution)/shard_map/psum | solution.py:13
  198.9 6.6 copy-start.3
  229.4 142.7 %reduce-scatter.3.cloned.1.call-start = ((), (), s32[]{:S(2)}) async-start(), calls=%async_computation.3 | async-start | bytes 4718592 | tf_op jit(solution)/shard_map/reduce_scatter | solution.py:28
  335.3 72.8 %all-gather.7.cloned.1.call-start = ((), (), s32[]{:S(2)}) async-start(), calls=%async_computation.4 | async-start | bytes 4718592 | tf_op jit(solution)/shard_map/all_gather | solution.py:29
  372.2 185.1 %all-gather.13.cloned.1.call-start = ((), (), s32[]{:S(2)}) async-start(), calls=%async_computation.9 | async-start | bytes 9437184 | tf_op jit(solution)/shard_map/all_gather | solution.py:8
  507.6 232.5 %all-reduce.6.cloned.1.call-start = ((), (), s32[]{:S(2)}) async-start(), calls=%async_computation.5 | async-start | bytes 8388608 | tf_op jit(solution)/shard_map/psum | solution.py:13
  606.0 6.6 copy-start.2
  636.8 142.7 %reduce-scatter.5.cloned.1.call-start = ((), (), s32[]{:S(2)}) async-start(), calls=%async_computation.6 | async-start | bytes 4718592 | tf_op jit(solution)/shard_map/reduce_scatter | solution.py:28
  742.5 72.9 %all-gather.9.cloned.1.call-start = ((), (), s32[]{:S(2)}) async-start(), calls=%async_computation.7 | async-start | bytes 4718592 | tf_op jit(solution)/shard_map/all_gather | solution.py:29
  815.5 17.0 %copy-start = (f32[4,512,2,512]{3,1,2,0:T(8,128)S(1)}, f32[4,512,2,512]{3,1,2,0:T(8,128)}, u32[]{:S(2)}) copy-start(f32[4,512,2,512]{3,1,2,0:T(8,128)} %select_dynamic-update-slice_fusion) | copy-start | bytes 25165828
  815.5 17.0 %copy-start.1 = (f32[4,512,512]{2,1,0:T(8,128)S(1)}, f32[4,512,512]{2,1,0:T(8,128)}, u32[]{:S(2)}) copy-start(f32[4,512,512]{2,1,0:T(8,128)} %all-reduce.4.cloned.1.call-done) | copy-start | bytes 12582916
Sparse Core Ops, SparseCore 0:
  96.1 53.2 all-gather.10
  229.5 103.1 all-reduce.3
  335.4 36.7 reduce-scatter.2
  373.7 34.2 all-gather.6
  507.7 49.6 all-gather.12
  636.9 103.1 all-reduce.5
  742.7 36.7 reduce-scatter.4
  781.2 34.2 all-gather.8
where the time goes:
time: 883 us; the launch traced here: 873 us
  waiting for transfers between devices  419 us (47%)
  other arithmetic  278 us (31%)
  matrix products  85.5 us (10%)
  local copies, waits for them, and re-layouts  69.8 us (8%)
  between operations  20.2 us (2%)
    psum x2, waiting for transfers between devices, from_root(): return lax.psum(kept, axis)  207 us
    another operation x29, other arithmetic, factor_panel(): factor = picked(jnp.linalg.cholesky(diag_raw), 'row', owner_row)  158 us
    all_gather x2, waiting for transfers between devices, picked(): lax.all_gather(x, axis)  85.5 us
    another operation x5, other arithmetic, factor_panel(): jax.scipy.linalg.solve_triangular(factor, flat_rows.T, lower=True)  82 us
    reduce_scatter x2, waiting for transfers between devices, broadcast_by_parts(): own = lax.psum_scatter(padded, axis, scatter_dimension=0, tiled=True)  73.7 us
    all_gather x2, waiting for transfers between devices, broadcast_by_parts(): lax.all_gather(own, axis, axis=0, tiled=True)[:len(lines)].reshape(x.shape)  53.5 us
    another operation x14, matrix products, factor_panel(): jax.scipy.linalg.solve_triangular(factor, flat_rows.T, lower=True)  35.7 us
    dot_general x2, matrix products, update(): lax.dot_general(left_panel, right_panel, (((1,), (1,)), ((), ())), precis...  35.1 us
  transfers between devices with their start and end apart: 8, of which 8 were waited for; matrix products, arithmetic and copies ran while one was open for 4% of the time, Pallas kernels for 0%

commit v1 on v0

--- a/solution.py
+++ b/solution.py
@@ -10,7 +10,11 @@
 
 def from_root(value, axis, source):
     kept = jnp.where(lax.axis_index(axis) == source, value, 0).astype(value.dtype)
-    return lax.psum(kept, axis)
+
+    def step_on_the_counts(u_in):
+        return jnp.sum(lax.all_gather(u_in, axis), axis=0)
+
+    return step_on_the_counts(kept)
 
 
 def padded_to(lines, length):

time: 883 us -> 1500 us (1.70)
  waiting for transfers between devices: 419 us -> 937 us
  other arithmetic: 278 us -> 322 us
  local copies, waits for them, and re-layouts: 69.8 us -> 107 us
    all_gather x0 -> x2, waiting for transfers between devices: none -> 737 us  [step_on_the_counts(): return jnp.sum(lax.all_gather(u_in, axis), axis=0)]
    psum x2 -> x0, waiting for transfers between devices: 207 us -> none  [from_root(): return lax.psum(kept, axis)]
    reduce_sum x0 -> x2, other arithmetic: none -> 46.2 us  [step_on_the_counts(): return jnp.sum(lax.all_gather(u_in, axis), axis=0)]
    dot_general x2, matrix products: 35.1 us -> 62.2 us  [update(): lax.dot_general(left_panel, right_panel, (((1,), (1,)), ((), ())), precis...]
  transfers between devices with their start and end apart: 8 -> 8, of which waited for: 8 -> 8; matrix products, arithmetic and copies ran while one was open for 4% -> 3% of each run, Pallas kernels for 0% -> 0%
where the time goes in v1:
time: 1500 us; the launch traced here: 1490 us
  waiting for transfers between devices  937 us (62%)
  other arithmetic  322 us (21%)
  local copies, waits for them, and re-layouts  107 us (7%)
  matrix products  99.1 us (7%)
  between operations  20.1 us (1%)
    all_gather x2, waiting for transfers between devices, step_on_the_counts(): return jnp.sum(lax.all_gather(u_in, axis), axis=0)  737 us
    another operation x29, other arithmetic, factor_panel(): factor = picked(jnp.linalg.cholesky(diag_raw), 'row', owner_row)  158 us
    another operation x5, other arithmetic, factor_panel(): jax.scipy.linalg.solve_triangular(factor, flat_rows.T, lower=True)  81.6 us
    all_gather x2, waiting for transfers between devices, picked(): lax.all_gather(x, axis)  74.1 us
    reduce_scatter x2, waiting for transfers between devices, broadcast_by_parts(): own = lax.psum_scatter(padded, axis, scatter_dimension=0, tiled=True)  73.1 us
    dot_general x2, matrix products, update(): lax.dot_general(left_panel, right_panel, (((1,), (1,)), ((), ())), precis...  62.2 us
    all_gather x2, waiting for transfers between devices, broadcast_by_parts(): lax.all_gather(own, axis, axis=0, tiled=True)[:len(lines)].reshape(x.shape)  53.4 us
    reduce_sum x2, other arithmetic, step_on_the_counts(): return jnp.sum(lax.all_gather(u_in, axis), axis=0)  46.2 us
  transfers between devices with their start and end apart: 8, of which 8 were waited for; matrix products, arithmetic and copies ran while one was open for 3% of the time, Pallas kernels for 0%

profile of v1, /device:TPU:1, one launch (start us, length us, event | category | flops | bytes accessed | tf_op | source)
XLA Modules:
  0.0 1486.1 jit_solution(1432974212987800538)
XLA Ops:
  11.3 11.7 cholesky.286
  33.7 11.7 cholesky.305
  56.1 11.7 cholesky.326
  78.9 11.7 cholesky.343
  114.7 34.4 %all-gather.17.cloned.1.call-done = f32[4096,512]{1,0:T(8,128)} async-done(((f32[512,512]{1,0:T(8,128)}), f32[4096,512]{1,0:T(8,128)}) %all-gather.17.cloned.1.call-update) | async-done | bytes 8388624 | tf_op jit(solution)/shard_map/all_gather | solution.py:8
  158.8 39.3 %custom-call.30 = f32[4,128,128]{1,2,0:T(8,128)S(1)} custom-call(f32[4,128,128]{2,1,0:T(8,128)S(1)} %get-tuple-element.21), custom_call_target="InvertDiagBlocksLowerTriangular" | custom-call | tf_op jit(solution)/shard_map/jit(_solve_triangular)/triangular_solve | solution.py:66
  222.2 368.3 %all-gather.9.cloned.1.call-done = f32[16,4,512,512]{3,2,1,0:T(8,128)} async-done(((f32[1,4,512,512]{3,2,1,0:T(8,128)}), f32[16,4,512,512]{3,2,1,0:T(8,128)}) %all-gather.9.cloned.1.call-update) | async-done | bytes 67108880 | tf_op jit(solution)/shard_map/all_gather | solution.py:15
  590.6 23.1 %reduce_sum.18 = f32[4,512,512]{2,1,0:T(8,128)} reduce(f32[16,4,512,512]{3,2,1,0:T(8,128)} %all-gather.9.cloned.1.call-done, f32[]{:T(128)} %constant.302.clone.1), dimensions={0}, to_apply=%region_8.11 | reduce | flops 15728640 | bytes 71303168 | tf_op jit(solution)/shard_map/reduce_sum | solution.py:15
  623.9 36.5 %reduce-scatter.3.cloned.1.call-done = f32[256,512]{0,1:T(8,128)} async-done(((f32[2048,512]{0,1:T(8,128)}), f32[256,512]{0,1:T(8,128)}) %reduce-scatter.3.cloned.1.call-update) | async-done | bytes 524304 | tf_op jit(solution)/shard_map/reduce_scatter | solution.py:32
  672.1 24.2 %all-gather.11.cloned.1.call-done = f32[2048,512]{0,1:T(8,128)} async-done(((f32[256,512]{0,1:T(8,128)}), f32[2048,512]{0,1:T(8,128)}) %all-gather.11.cloned.1.call-update) | async-done | bytes 4194320 | tf_op jit(solution)/shard_map/all_gather | solution.py:33
  701.7 11.0 bitcast_dynamic-update-slice_fusion.2
  715.8 11.7 cholesky.358
  738.2 11.7 cholesky.377
  762.2 11.7 cholesky.398
  784.9 11.7 cholesky.415
  811.3 39.6 %all-gather.19.cloned.1.call-done = f32[4096,512]{1,0:T(8,128)} async-done(((f32[512,512]{1,0:T(8,128)}), f32[4096,512]{1,0:T(8,128)}) %all-gather.19.cloned.1.call-update) | async-done | bytes 8388624 | tf_op jit(solution)/shard_map/all_gather | solution.py:8
  860.5 39.3 %custom-call.34 = f32[4,128,128]{1,2,0:T(8,128)S(1)} custom-call(f32[4,128,128]{2,1,0:T(8,128)S(1)} %get-tuple-element.22), custom_call_target="InvertDiagBlocksLowerTriangular" | custom-call | tf_op jit(solution)/shard_map/jit(_solve_triangular)/triangular_solve | solution.py:66
  923.7 368.4 %all-gather.13.cloned.1.call-done = f32[16,4,512,512]{3,2,1,0:T(8,128)} async-done(((f32[1,4,512,512]{3,2,1,0:T(8,128)}), f32[16,4,512,512]{3,2,1,0:T(8,128)}) %all-gather.13.cloned.1.call-update) | async-done | bytes 67108880 | tf_op jit(solution)/shard_map/all_gather | solution.py:15
  1292.1 23.1 %reduce_sum.19 = f32[4,512,512]{2,1,0:T(8,128)} reduce(f32[16,4,512,512]{3,2,1,0:T(8,128)} %all-gather.13.cloned.1.call-done, f32[]{:T(128)} %constant.302.clone.1), dimensions={0}, to_apply=%region_10.13 | reduce | flops 15728640 | bytes 71303168 | tf_op jit(solution)/shard_map/reduce_sum | solution.py:15
  1328.8 36.5 %reduce-scatter.5.cloned.1.call-done = f32[256,512]{1,0:T(8,128)} async-done(((f32[2048,512]{1,0:T(8,128)}), f32[256,512]{1,0:T(8,128)}) %reduce-scatter.5.cloned.1.call-update) | async-done | bytes 524304 | tf_op jit(solution)/shard_map/reduce_scatter | solution.py:32
  1372.3 29.1 %all-gather.15.cloned.1.call-done = f32[2048,512]{1,0:T(8,128)} async-done(((f32[256,512]{1,0:T(8,128)}), f32[2048,512]{1,0:T(8,128)}) %all-gather.15.cloned.1.call-update) | async-done | bytes 4194320 | tf_op jit(solution)/shard_map/all_gather | solution.py:33
  1401.4 30.7 %fusion = f32[4,512,2,512]{3,1,2,0:T(8,128)S(1)} fusion(f32[4,512,512,1]{1,0,2,3:T(4,128)} %bitcast.168, f32[2,2,512,512]{3,2,1,0:T(8,128)} %bitcast.188, s32[]{:T(128)S(6)} %select_n.224), kind=kOutput, calls=%fused_computation.8 | convolution fusion | flops 12884901888 | bytes 14680068 | tf_op jit(solution)/shard_map/dot_general | solution.py:41
  1432.1 31.6 %subtract_subtract_fusion = f32[4,512,2,512]{3,1,2,0:T(8,128)} fusion(f32[4,512,2,512]{3,1,2,0:T(8,128)S(1)} %fusion, f32[4,512,2,512]{3,1,2,0:T(8,128)S(1)} %copy-done, f32[4,512,512,1]{1,0,2,3:T(4,128)S(1)} %bitcast.167, f32[2,2,512,512]{3,2,1,0:T(8,128)} %bitcast.187, s32[]{:T(128)S(6)} %select_n.224, pred[2]{0:T(512)(128)(4,1)S(1)} %iota_compare_fusion.3), kind=kOutput, calls=%fused_computation.4 | convolution fusion | flops 12889620480 | bytes 31457286 | tf_op jit(solution)/shard_map/dot_general | solution.py:41
  1463.7 15.4 %copy.43 = f32[4,512,2,512]{3,2,1,0:T(2,128)} copy(f32[4,512,2,512]{3,1,2,0:T(8,128)} %subtract_subtract_fusion) | data formatting | bytes 16777216 | tf_op jit(solution)/shard_map/sub | solution.py:48
  (144 shorter events, 237.8 us)
Async XLA Ops:
  6.5 142.6 %all-gather.17.cloned.1.call-start = ((), (), s32[]{:S(2)}) async-start(), calls=%async_computation.8 | async-start | bytes 9437184 | tf_op jit(solution)/shard_map/all_gather | solution.py:8
  95.7 494.9 %all-gather.9.cloned.1.call-start = ((), (), s32[]{:S(2)}) async-start(), calls=%async_computation.2 | async-start | bytes 71303168 | tf_op jit(solution)/shard_map/all_gather | solution.py:15
  198.2 5.7 copy-start.2
  222.2 438.3 %reduce-scatter.3.cloned.1.call-start = ((), (), s32[]{:S(2)}) async-start(), calls=%async_computation.3 | async-start | bytes 4718592 | tf_op jit(solution)/shard_map/reduce_scatter | solution.py:32
  623.9 72.4 %all-gather.11.cloned.1.call-start = ((), (), s32[]{:S(2)}) async-start(), calls=%async_computation.4 | async-start | bytes 4718592 | tf_op jit(solution)/shard_map/all_gather | solution.py:33
  660.5 190.4 %all-gather.19.cloned.1.call-start = ((), (), s32[]{:S(2)}) async-start(), calls=%async_computation.9 | async-start | bytes 9437184 | tf_op jit(solution)/shard_map/all_gather | solution.py:8
  801.2 490.9 %all-gather.13.cloned.1.call-start = ((), (), s32[]{:S(2)}) async-start(), calls=%async_computation.5 | async-start | bytes 71303168 | tf_op jit(solution)/shard_map/all_gather | solution.py:15
  899.8 5.7 copy-start.3
  923.7 441.7 %reduce-scatter.5.cloned.1.call-start = ((), (), s32[]{:S(2)}) async-start(), calls=%async_computation.6 | async-start | bytes 4718592 | tf_op jit(solution)/shard_map/reduce_scatter | solution.py:32
  1328.8 72.6 %all-gather.15.cloned.1.call-start = ((), (), s32[]{:S(2)}) async-start(), calls=%async_computation.7 | async-start | bytes 4718592 | tf_op jit(solution)/shard_map/all_gather | solution.py:33
  1401.4 30.7 %copy-start = (f32[4,512,2,512]{3,1,2,0:T(8,128)S(1)}, f32[4,512,2,512]{3,1,2,0:T(8,128)}, u32[]{:S(2)}) copy-start(f32[4,512,2,512]{3,1,2,0:T(8,128)} %select_dynamic-update-slice_fusion) | copy-start | bytes 25165828
  1401.4 30.7 %copy-start.1 = (f32[4,512,512]{1,0,2:T(4,128)S(1)}, f32[4,512,512]{1,0,2:T(4,128)}, u32[]{:S(2)}) copy-start(f32[4,512,512]{1,0,2:T(4,128)} %copy.59) | copy-start | bytes 12582916
Sparse Core Ops, SparseCore 0:
  95.8 53.2 all-gather.16
  222.3 368.2 all-gather.8
  624.0 36.4 reduce-scatter.2
  662.0 34.2 all-gather.10
  801.3 49.6 all-gather.18
  923.8 368.2 all-gather.12
  1328.9 36.4 reduce-scatter.4
  1367.1 34.2 all-gather.14
